TPU v7x, 32 devices: a whole 2x2x4 slice. The times are simulated.
32 devices in a mesh: grp: 2 (over y), kvp: 4 (over x, core), tp: 4 (over z).
Axes of the slice: x: 2, y: 2, z: 4, core: 2. Of those that a mesh axis runs over, the one named last changes fastest.
Arguments:
- normed: bfloat16 [512, 6144], P('grp', 'kvp'), parts along dimension 0, may hold values from -6 to 6
- w_query: bfloat16 [6144, 6144], P('kvp', 'tp'), may hold values from -0.078125 to 0.078125
- w_key: bfloat16 [6144, 1024], P('kvp', 'tp'), may hold values from -0.078125 to 0.078125
- w_value: bfloat16 [6144, 1024], P('kvp', 'tp'), may hold values from -0.078125 to 0.078125
- w_out: bfloat16 [6144, 6144], P('tp', 'kvp'), may hold values from -0.078125 to 0.078125
- key_cache: bfloat16 [8, 1024, 128, 128], P('tp', ('grp', 'kvp')), parts along dimension 1, may hold values from -128 to 128
- value_cache: bfloat16 [8, 1024, 128, 128], P('tp', ('grp', 'kvp')), parts along dimension 1, may hold values from -6 to 6
- lengths: int32 [512], P('grp'), parts along dimension 0, may hold values from 1 to 12288, as said below
- page_table: int32 [512, 96], P('grp'), parts along dimension 0, may hold values from -1 to 511, as said below
Outputs:
- attended: bfloat16 [512, 6144], P(('grp', 'tp'), 'kvp'), parts along dimension 0
There are 2 independent parts, one for each index of `grp`. A program takes and returns all parts, laid end to end along the dimension named above; an argument that names none is the same for every part. Nothing has to cross between parts.
Inputs may be any that keep to these rules, and one draw needn't show every extreme that they name: `lengths`: every request has at least one cached token; the longest request fills all 96 entries of its page table. `page_table`: entry [b, j] is a page index exactly when j < ceil(lengths[b] / 128), else -1; no page is named twice. Index kvp = i holds pages i * 128 to (i + 1) * 128 - 1; the pages in use are spread unevenly over kvp.
All inputs are finite; a program needn't handle non-finite values.
Results may differ from a plain program's by a relative error of at most 0.012.
Values may be sent and summed in bfloat16 or wider, within the bound.
A program may use at most 64 MiB of HBM per device.

v0:
```python
import jax
import jax.numpy as jnp
from jax import lax
from jax.sharding import PartitionSpec as P

ROPE_BASE = 1000000.0
NEG = -1e30
TWO_PI_HIGH = 6.28125
TWO_PI_LOW = 0.0019353071795864768


def rotate(x, pos):
    width = x.shape[-1]
    half = width // 2
    freq = ROPE_BASE ** (-(2.0 * jnp.arange(half, dtype=jnp.float32)) / width)
    coarse = lax.optimization_barrier(freq.astype(jnp.bfloat16)).astype(jnp.float32)
    fine = freq - coarse
    pos_e = pos[..., None]
    exact = pos_e * coarse
    turns = jnp.floor(exact / TWO_PI_HIGH)
    angle = exact - turns * TWO_PI_HIGH - turns * TWO_PI_LOW + pos_e * fine
    cosine = jnp.cos(angle)
    sine = jnp.sin(angle)
    first = x[..., :half]
    second = x[..., half:]
    return jnp.concatenate(
        [first * cosine - second * sine, second * cosine + first * sine], axis=-1
    )


def source_merge(received):
    marks, totals, accs = received
    top = jnp.max(marks, axis=0)
    weight = jnp.exp(marks - top[None])
    return (top, jnp.sum(weight * totals, axis=0), jnp.sum(weight[..., None] * accs, axis=0))


def finish(top, total, acc, q_rows, k_rows, v_rows, scale):
    s_new = jnp.einsum("bhgd,bhd->bhg", q_rows, k_rows, preferred_element_type=jnp.float32) * scale
    peak = jnp.maximum(top, s_new)
    w_old = jnp.exp(top - peak)
    w_new = jnp.exp(s_new - peak)
    total = w_old * total + w_new
    acc = w_old[..., None] * acc + w_new[..., None] * v_rows.astype(jnp.float32)[:, :, None, :]
    out = (acc / total[..., None]).astype(jnp.bfloat16)
    return out.reshape(out.shape[0], -1)


def body(normed, w_query, w_key, w_value, w_out, key_cache, value_cache, lengths, page_table):
    batch = normed.shape[0]
    kv_local = key_cache.shape[0]
    pages = key_cache.shape[1]
    page = key_cache.shape[2]
    head_dim = key_cache.shape[3]
    group = w_query.shape[1] // (kv_local * head_dim)
    blocks_max = page_table.shape[1]
    scale = head_dim ** (-0.5)
    rank = lax.axis_index("kvp")
    spread = lax.axis_size("kvp")
    rows = batch // spread
    start = rank * rows
    part_q = jnp.dot(normed, w_query, preferred_element_type=jnp.float32)
    part_k = jnp.dot(normed, w_key, preferred_element_type=jnp.float32)
    part_v = jnp.dot(normed, w_value, preferred_element_type=jnp.float32)
    position = lengths.astype(jnp.float32)
    q_share, k_share, v_share = (
        lax.psum_scatter(part_q, "kvp", scatter_dimension=0, tiled=True),
        lax.psum_scatter(part_k, "kvp", scatter_dimension=0, tiled=True),
        lax.psum_scatter(part_v, "kvp", scatter_dimension=0, tiled=True),
    )
    pos_share = lax.dynamic_slice_in_dim(position, start, rows, 0)
    q_part = rotate(
        q_share.reshape(rows, kv_local, group, head_dim), pos_share[:, None, None]
    ).astype(jnp.bfloat16)
    k_rows = rotate(k_share.reshape(rows, kv_local, head_dim), pos_share[:, None]).astype(
        jnp.bfloat16
    )
    v_rows = v_share.reshape(rows, kv_local, head_dim).astype(jnp.bfloat16)
    q_rot = lax.all_gather(q_part, "kvp", axis=0, tiled=True)
    slot_ids = rank * pages + jnp.arange(pages, dtype=jnp.int32)
    hits = page_table[:, :, None] == slot_ids[None, None, :]
    present = jnp.any(hits, axis=(0, 1))
    request_ids = jnp.arange(batch, dtype=jnp.int32)
    owner = jnp.sum(jnp.where(hits, request_ids[:, None, None], 0), axis=(0, 1))
    block = jnp.sum(
        jnp.where(hits, jnp.arange(blocks_max, dtype=jnp.int32)[None, :, None], 0), axis=(0, 1)
    )
    q_owned = q_rot[owner]
    token_pos = block[:, None] * page + jnp.arange(page, dtype=jnp.int32)[None, :]
    valid = present[:, None] & (token_pos < lengths[owner][:, None])
    scores = (
        jnp.einsum("phgd,hptd->phgt", q_owned, key_cache, preferred_element_type=jnp.float32)
        * scale
    )
    scores = jnp.where(valid[:, None, None, :], scores, NEG)
    slot_top = jnp.max(scores, axis=-1)
    weights = jnp.where(valid[:, None, None, :], jnp.exp(scores - slot_top[..., None]), 0.0)
    slot_total = jnp.sum(weights, axis=-1)
    slot_acc = jnp.einsum(
        "phgt,hptd->phgd",
        weights.astype(jnp.bfloat16),
        value_cache,
        preferred_element_type=jnp.float32,
    )
    belongs = (owner[None, :] == request_ids[:, None]) & present[None, :]
    mask = belongs[:, :, None, None]
    top = jnp.max(jnp.where(mask, slot_top[None], NEG), axis=1)
    factor = jnp.where(mask, jnp.exp(slot_top[None] - top[:, None]), 0.0)
    total = jnp.sum(factor * slot_total[None], axis=1)
    acc = jnp.einsum("bphg,phgd->bhgd", factor, slot_acc, precision=lax.Precision.HIGHEST)
    top, total, acc = source_merge(
        (
            lax.all_to_all(top[None], "kvp", split_axis=1, concat_axis=0, tiled=True),
            lax.all_to_all(total[None], "kvp", split_axis=1, concat_axis=0, tiled=True),
            lax.all_to_all(acc[None], "kvp", split_axis=1, concat_axis=0, tiled=True),
        )
    )
    q_rows = lax.dynamic_slice_in_dim(q_rot, start, rows, 0)
    head_out = finish(top, total, acc, q_rows, k_rows, v_rows, scale)
    terms = jnp.dot(
        lax.all_gather(head_out, "kvp", axis=0, tiled=True),
        w_out,
        preferred_element_type=jnp.float32,
    )
    return lax.psum_scatter(terms, "tp", scatter_dimension=0, tiled=True).astype(jnp.bfloat16)


def solution(mesh):
    return jax.shard_map(
        body,
        mesh=mesh,
        in_specs=(
            P("grp", "kvp"),
            P("kvp", "tp"),
            P("kvp", "tp"),
            P("kvp", "tp"),
            P("tp", "kvp"),
            P("tp", ("grp", "kvp"), None, None),
            P("tp", ("grp", "kvp"), None, None),
            P("grp"),
            P("grp", None),
        ),
        out_specs=P(("grp", "tp"), "kvp"),
        check_vma=False,
    )
```

profile of v0, /device:TPU:0, one launch (start us, length us, event | category | flops | bytes accessed | tf_op | source)
XLA Modules:
  0.0 187.5 jit_solution(7497890433573598699)
XLA Ops:
  6.5 1.1 copy-done
  7.7 2.2 %fusion.49 = f32[256,256]{1,0:T(8,128)} fusion(bf16[256,1536]{1,0:T(8,128)(2,1)S(1)} %copy-done, bf16[1536,256]{1,0:T(8,128)(2,1)} %param.11), kind=kOutput, calls=%fused_computation.77 | convolution fusion | flops 201326592 | bytes 1835008 | tf_op jit(solution)/shard_map/dot_general | solution.py:63
  9.9 4.9 %fusion.48 = f32[256,1536]{1,0:T(8,128)} fusion(bf16[256,1536]{1,0:T(8,128)(2,1)S(1)} %copy-done, bf16[1536,1536]{1,0:T(8,128)(2,1)} %param.10), kind=kOutput, calls=%fused_computation.76 | convolution fusion | flops 1207959552 | bytes 7077888 | tf_op jit(solution)/shard_map/dot_general | solution.py:62
  14.9 1.0 copy-done.2
  15.9 1.1 fusion.50
  17.2 4.6 %fusion.1 = (s32[128]{0:T(128)S(1)}, s32[128]{0:T(128)S(1)}) fusion(s32[128]{0:T(128)S(1)} %iota_add_fusion, s32[256,96]{1,0:T(8,128)S(1)} %copy.63), kind=kLoop, calls=%fused_computation.6 | loop fusion | flops 15728384 | bytes 99840 | tf_op jit(solution)/shard_map/reduce_sum | solution.py:85
  21.8 4.5 %compare_reduce_fusion = pred[128]{0:T(512)(128)(4,1)S(1)} fusion(s32[128]{0:T(128)S(1)} %iota_add_fusion, s32[256,96]{1,0:T(8,128)S(1)} %copy.63), kind=kLoop, calls=%fused_computation.3 | loop fusion | flops 6291328 | bytes 98944 | tf_op jit(solution)/shard_map/reduce_or | solution.py:82
  26.3 1.3 gather_fusion
  27.9 0.2 fusion.37
  28.1 4.7 %reduce-scatter.7.cloned.1.call-done = f32[64,256]{1,0:T(8,128)} async-done(((f32[256,256]{1,0:T(8,128)}), f32[64,256]{1,0:T(8,128)}) %reduce-scatter.7.cloned.1.call-update) | async-done | bytes 65552 | tf_op jit(solution)/shard_map/reduce_scatter | solution.py:68
  32.8 0.9 reshape.362
  33.7 29.7 %reduce-scatter.5.cloned.1.call-done = f32[64,1536]{1,0:T(8,128)} async-done(((f32[256,1536]{1,0:T(8,128)}), f32[64,1536]{1,0:T(8,128)}) %reduce-scatter.5.cloned.1.call-update) | async-done | bytes 393232 | tf_op jit(solution)/shard_map/reduce_scatter | solution.py:67
  63.4 1.1 reshape.361
  64.6 0.2 subtract_convert_fusion
  64.8 0.2 pad_maximum_fusion
  65.2 8.0 %all_gather.6 = bf16[256,2,6,128]{3,1,2,0:T(2,128)(2,1)S(1)} all-gather(bf16[64,2,6,128]{3,1,2,0:T(2,128)(2,1)S(1)} %copy.64), channel_id=1, replica_groups=mesh['grp'=2,'kvp'=4,'tp'=4] {'kvp'}, dimensions={0}, use_global_device_ids=true | all-gather | bytes 983040 | tf_op jit(solution)/shard_map/all_gather | solution.py:79
  73.2 1.4 gather_fusion.1
  74.6 7.0 %fusion.47 = (f32[128,2,6]{2,1,0:T(2,128)S(1)}, f32[128,2,6,128]{3,2,1,0:T(8,128)S(1)}) fusion(bf16[2,128,128,128]{3,2,1,0:T(8,128)(2,1)} %param.14, bf16[128,2,6,128]{3,1,2,0:T(2,128)(2,1)S(1)} %gather_fusion.1, pred[128,128]{1,0:T(8,128)(4,1)S(1)} %fusion.30), kind=kOutput, calls=%fused_computation.75 | convolution fusion | flops 50919936 | bytes 9590784 | tf_op jit(solution)/shard_map/phgd,hptd->phgt/dot_general | solution.py:92
  81.7 0.8 fusion.14
  82.6 0.5 select_reduce_fusion
  83.1 0.9 multiply_reduce_fusion
  84.0 0.2 copy.79
  84.2 1.0 reshape.384
  85.1 3.3 %all-to-all-start.2 = ((f32[4,1,768]{2,1,0:T(1,128)}), f32[4,1,768]{2,1,0:T(1,128)S(1)}, u32[]{:S(2)}, u32[]{:S(2)}) async-start(f32[4,1,768]{2,1,0:T(1,128)} %reshape.384), calls=%async_computation.5 | async-start | bytes 24576 | tf_op jit(solution)/shard_map/all_to_all | solution.py:114
  88.4 6.7 %fusion.2 = f32[128,2,6,128]{3,2,1,0:T(8,128)} fusion(bf16[2,128,128,128]{3,2,1,0:T(8,128)(2,1)} %param.15, f32[128,2,6,128]{3,2,1,0:T(8,128)S(1)} %get-tuple-element.19, f32[128,2,6]{2,1,0:T(2,128)S(1)} %get-tuple-element.18, pred[128,128]{1,0:T(8,128)(4,1)S(1)} %fusion.30), kind=kOutput, calls=%fused_computation.7 | convolution fusion | flops 50921472 | bytes 9984000 | tf_op jit(solution)/shard_map/phgt,hptd->phgd/dot_general | solution.py:99
  95.1 0.2 copy.68
  95.3 1.0 reshape.382
  96.2 3.4 %all-to-all-start = ((f32[4,1,768]{2,1,0:T(1,128)}), f32[4,1,768]{2,1,0:T(1,128)S(1)}, u32[]{:S(2)}, u32[]{:S(2)}) async-start(f32[4,1,768]{2,1,0:T(1,128)} %reshape.382), calls=%async_computation.1 | async-start | bytes 24576 | tf_op jit(solution)/shard_map/all_to_all | solution.py:113
  99.7 3.4 %fusion.7 = f32[1,256,2,6,128]{1,4,3,2,0:T(8,128)S(1)} fusion(f32[128,2,6,128]{3,2,1,0:T(8,128)} %fusion.2, f32[256,2,6]{0,2,1:T(8,128)S(1)} %select_reduce_fusion, f32[128,2,6]{0,2,1:T(8,128)S(1)} %copy.67, pred[256,128]{1,0:T(8,128)(4,1)S(1)} %fusion.28), kind=kOutput, calls=%fused_computation.16 | convolution fusion | flops 604766208 | bytes 2410496 | tf_op jit(solution)/shard_map/bphg,phgd->bhgd/dot_general | solution.py:110
  103.1 2.2 %copy.74 = f32[1,256,2,6,128]{4,2,3,0,1:T(2,128)} copy(f32[1,256,2,6,128]{1,4,3,2,0:T(8,128)S(1)} %fusion.7) | data formatting | bytes 3145728 | tf_op jit(solution)/shard_map/broadcast_in_dim | solution.py:115
  105.2 3.6 %all-to-all-start.1 = ((f32[1,256,2,6,128]{4,2,3,0,1:T(2,128)}), f32[1,256,2,6,128]{4,2,3,0,1:T(2,128)S(1)}, u32[]{:S(2)}, u32[]{:S(2)}) async-start(f32[1,256,2,6,128]{4,2,3,0,1:T(2,128)} %copy.74), calls=%async_computation.3 | async-start | bytes 3145728 | tf_op jit(solution)/shard_map/all_to_all | solution.py:115
  108.9 0.2 subtract_convert_fusion.1
  109.2 0.8 copy_bitcast_fusion
  110.2 0.3 fusion.26
  110.5 0.5 broadcast.314
  111.1 0.7 reduce
  111.7 0.4 reshape.385
  112.3 0.7 reduce.1
  113.0 0.4 reshape.383
  113.5 0.2 reduce_max.29
  113.9 14.9 %all-to-all-done.1 = f32[1,256,2,6,128]{4,2,3,0,1:T(2,128)S(1)} async-done(((f32[1,256,2,6,128]{4,2,3,0,1:T(2,128)}), f32[1,256,2,6,128]{4,2,3,0,1:T(2,128)S(1)}, u32[]{:S(2)}, u32[]{:S(2)}) %all-to-all-start.1) | async-done | bytes 1572896 | tf_op jit(solution)/shard_map/all_to_all | solution.py:115
  129.0 0.5 multiply_reduce_fusion.1
  129.4 0.4 divide_convert_fusion
  130.0 0.2 convert_element_type.52
  130.2 7.9 %all_gather.7 = bf16[256,1536]{1,0:T(8,128)(2,1)S(1)} all-gather(bf16[64,1536]{1,0:T(8,128)(2,1)S(1)} %convert_element_type.52), channel_id=1, replica_groups=mesh['grp'=2,'kvp'=4,'tp'=4] {'kvp'}, dimensions={0}, use_global_device_ids=true | all-gather | bytes 983040 | tf_op jit(solution)/shard_map/all_gather | solution.py:121
  138.1 4.9 %fusion.51 = f32[256,1536]{1,0:T(8,128)} fusion(bf16[256,1536]{1,0:T(8,128)(2,1)S(1)} %all_gather.7, bf16[1536,1536]{1,0:T(8,128)(2,1)} %param.13), kind=kOutput, calls=%fused_computation.79 | convolution fusion | flops 1207959552 | bytes 7077888 | tf_op jit(solution)/shard_map/dot_general | solution.py:120
  143.0 36.3 %reduce-scatter.11.cloned.1.call-done = f32[64,1536]{1,0:T(8,128)} async-done(((f32[256,1536]{1,0:T(8,128)}), f32[64,1536]{1,0:T(8,128)}) %reduce-scatter.11.cloned.1.call-update) | async-done | bytes 393232 | tf_op jit(solution)/shard_map/reduce_scatter | solution.py:125
  179.3 1.7 convert_element_type.53
  (45 shorter events, 2.0 us)
Async XLA Ops:
  6.5 1.1 copy-start
  6.5 26.3 %reduce-scatter.7.cloned.1.call-start = ((), (), s32[]{:S(2)}) async-start(), calls=%async_computation.8 | async-start | bytes 327680 | tf_op jit(solution)/shard_map/reduce_scatter | solution.py:68
  9.9 53.6 %reduce-scatter.5.cloned.1.call-start = ((), (), s32[]{:S(2)}) async-start(), calls=%async_computation.7 | async-start | bytes 1966080 | tf_op jit(solution)/shard_map/reduce_scatter | solution.py:67
  14.8 1.1 copy-start.2
  14.8 2.3 %copy-start.3 = (s32[256,96]{0,1:T(8,128)S(1)}, s32[256,96]{0,1:T(8,128)}, u32[]{:S(2)}) copy-start(s32[256,96]{0,1:T(8,128)} %param.17) | copy-start | bytes 294916
  14.8 11.5 %copy-start.1 = (s32[256]{0:T(256)S(1)}, s32[256]{0:T(256)}, u32[]{:S(2)}) copy-start(s32[256]{0:T(256)} %param.16) | copy-start | bytes 3076
  14.9 94.3 %reduce-scatter.9.cloned.1.call-start = ((), (), s32[]{:S(2)}) async-start(), calls=%async_computation.9 | async-start | bytes 327680 | tf_op jit(solution)/shard_map/reduce_scatter | solution.py:69
  85.1 11.1 %all-to-all-start.2 = ((f32[4,1,768]{2,1,0:T(1,128)}), f32[4,1,768]{2,1,0:T(1,128)S(1)}, u32[]{:S(2)}, u32[]{:S(2)}) async-start(f32[4,1,768]{2,1,0:T(1,128)} %reshape.384), calls=%async_computation.5 | async-start | bytes 24576 | tf_op jit(solution)/shard_map/all_to_all | solution.py:114
  96.2 9.0 %all-to-all-start = ((f32[4,1,768]{2,1,0:T(1,128)}), f32[4,1,768]{2,1,0:T(1,128)S(1)}, u32[]{:S(2)}, u32[]{:S(2)}) async-start(f32[4,1,768]{2,1,0:T(1,128)} %reshape.382), calls=%async_computation.1 | async-start | bytes 24576 | tf_op jit(solution)/shard_map/all_to_all | solution.py:113
  105.2 23.6 %all-to-all-start.1 = ((f32[1,256,2,6,128]{4,2,3,0,1:T(2,128)}), f32[1,256,2,6,128]{4,2,3,0,1:T(2,128)S(1)}, u32[]{:S(2)}, u32[]{:S(2)}) async-start(f32[1,256,2,6,128]{4,2,3,0,1:T(2,128)} %copy.74), calls=%async_computation.3 | async-start | bytes 3145728 | tf_op jit(solution)/shard_map/all_to_all | solution.py:115
  108.8 70.5 %reduce-scatter.11.cloned.1.call-start = ((), (), s32[]{:S(2)}) async-start(), calls=%async_computation.10 | async-start | bytes 1966080 | tf_op jit(solution)/shard_map/reduce_scatter | solution.py:125
Sparse Core Ops, SparseCore 0:
  10.0 22.7 reduce-scatter.6
  35.4 28.0 reduce-scatter.4
  65.9 20.0 reduce-scatter.8
  143.1 36.0 reduce-scatter.10
where the time goes:
time: 188 us; the launch traced here: 187 us
  waiting for transfers between devices  85.7 us (46%)
  matrix products  30.4 us (16%)
  other arithmetic  17.4 us (9%)
  blocking collectives  15.9 us (8%)
  local copies, waits for them, and re-layouts  14.2 us (8%)
  between operations  13.5 us (7%)
  starting transfers between devices  10.4 us (6%)
    reduce_scatter x1, waiting for transfers between devices, body(): lax.psum_scatter(terms, 'tp', scatter_dimension=0, tiled=True)  36.3 us
    reduce_scatter x1, waiting for transfers between devices, body(): lax.psum_scatter(part_q, 'kvp', scatter_dimension=0, tiled=True)  29.7 us
    all_to_all x1, waiting for transfers between devices, body(): lax.all_to_all(acc[None], 'kvp', split_axis=1, concat_axis=0, tiled=True)  14.9 us
    all_gather x1, blocking collectives, body(): q_rot = lax.all_gather(q_part, 'kvp', axis=0, tiled=True)  8.04 us
    all_gather x1, blocking collectives, body(): lax.all_gather(head_out, 'kvp', axis=0, tiled=True)  7.9 us
    dot_general x1, matrix products, body(): jnp.einsum('phgd,hptd->phgt', q_owned, key_cache, preferred_element_type=...  6.99 us
    dot_general x1, matrix products, body(): jnp.einsum('phgt,hptd->phgd', weights.astype(jnp.bfloat16), value_cache,...  6.71 us
    unnamed x14, local copies, waits for them, and re-layouts  5.09 us
  transfers between devices with their start and end apart: 7, of which 4 were waited for; matrix products, arithmetic and copies ran while one was open for 26% of the time, Pallas kernels for 0%

commit v1 on v0

--- a/solution.py
+++ b/solution.py
@@ -7,6 +7,12 @@
 NEG = -1e30
 TWO_PI_HIGH = 6.28125
 TWO_PI_LOW = 0.0019353071795864768
+
+
+def swap_blocks(array, name, split, join):
+    shards = jnp.split(array, lax.axis_size(name), axis=split)
+    incoming = lax.all_to_all(jnp.stack(shards), name, 0, 0)
+    return jnp.concatenate(incoming, axis=join)
 
 
 def rotate(x, pos):
@@ -112,7 +118,7 @@
         (
             lax.all_to_all(top[None], "kvp", split_axis=1, concat_axis=0, tiled=True),
             lax.all_to_all(total[None], "kvp", split_axis=1, concat_axis=0, tiled=True),
-            lax.all_to_all(acc[None], "kvp", split_axis=1, concat_axis=0, tiled=True),
+            swap_blocks(acc[None], "kvp", 1, 0),
         )
     )
     q_rows = lax.dynamic_slice_in_dim(q_rot, start, rows, 0)

time: 188 us -> 171 us (0.910)
  waiting for transfers between devices: 85.7 us -> 66.8 us
  matrix products: 30.4 us -> 26.1 us
  local copies, waits for them, and re-layouts: 14.2 us -> 17.5 us
  other arithmetic: 17.4 us -> 20.3 us
    reduce_scatter x1, waiting for transfers between devices: 29.7 us -> 17.5 us  [body(): lax.psum_scatter(part_q, 'kvp', scatter_dimension=0, tiled=True)]
    reduce_scatter x1, waiting for transfers between devices: 4.74 us -> 0.02 us  [body(): lax.psum_scatter(part_k, 'kvp', scatter_dimension=0, tiled=True)]
    another operation x0 -> x2, local copies, waits for them, and re-layouts: none -> 4.66 us  [swap_blocks(): incoming = lax.all_to_all(jnp.stack(shards), name, 0, 0)]
    another operation x2 -> x3, other arithmetic: 0.4 us -> 3.45 us  [the longest x1 3.05 us: swap_blocks(): incoming = lax.all_to_all(jnp.stack(shards), name, 0, 0)]
    broadcast_in_dim x1 -> x0, local copies, waits for them, and re-layouts: 2.17 us -> none  [body(): acc[None]]
    dot_general x1, matrix products: 6.71 us -> 4.73 us  [body(): jnp.einsum('phgt,hptd->phgd', weights.astype(jnp.bfloat16), value_cache,...]
    all_to_all x1, waiting for transfers between devices: 14.9 us -> 12.9 us  [swap_blocks(): incoming = lax.all_to_all(jnp.stack(shards), name, 0, 0)]
    unnamed x14 -> x19, local copies, waits for them, and re-layouts: 5.09 us -> 5.21 us
  transfers between devices with their start and end apart: 7 -> 7, of which waited for: 4 -> 3; matrix products, arithmetic and copies ran while one was open for 26% -> 29% of each run, Pallas kernels for 0% -> 0%
where the time goes in v1:
time: 171 us; the launch traced here: 170 us
  waiting for transfers between devices  66.8 us (39%)
  matrix products  26.1 us (15%)
  other arithmetic  20.3 us (12%)
  local copies, waits for them, and re-layouts  17.5 us (10%)
  blocking collectives  15.9 us (9%)
  between operations  13.5 us (8%)
  starting transfers between devices  10.4 us (6%)
    reduce_scatter x1, waiting for transfers between devices, body(): lax.psum_scatter(terms, 'tp', scatter_dimension=0, tiled=True)  36.3 us
    reduce_scatter x1, waiting for transfers between devices, body(): lax.psum_scatter(part_q, 'kvp', scatter_dimension=0, tiled=True)  17.5 us
    all_to_all x1, waiting for transfers between devices, swap_blocks(): incoming = lax.all_to_all(jnp.stack(shards), name, 0, 0)  12.9 us
    all_gather x1, blocking collectives, body(): q_rot = lax.all_gather(q_part, 'kvp', axis=0, tiled=True)  8.04 us
    all_gather x1, blocking collectives, body(): lax.all_gather(head_out, 'kvp', axis=0, tiled=True)  7.9 us
    dot_general x1, matrix products, body(): jnp.einsum('phgd,hptd->phgt', q_owned, key_cache, preferred_element_type=...  6.99 us
    unnamed x19, local copies, waits for them, and re-layouts  5.21 us
    dot_general x1, matrix products, body(): jnp.dot(lax.all_gather(head_out, 'kvp', axis=0, tiled=True), w_out, prefe...  4.89 us
  transfers between devices with their start and end apart: 7, of which 3 were waited for; matrix products, arithmetic and copies ran while one was open for 29% of the time, Pallas kernels for 0%

profile of v1, /device:TPU:0, one launch (start us, length us, event | category | flops | bytes accessed | tf_op | source)
XLA Modules:
  0.0 170.4 jit_solution(18085106761838069363)
XLA Ops:
  6.5 1.1 copy-done
  7.7 4.9 %fusion.49 = f32[256,1536]{1,0:T(8,128)} fusion(bf16[256,1536]{1,0:T(8,128)(2,1)S(1)} %copy-done, bf16[1536,1536]{1,0:T(8,128)(2,1)} %param.10), kind=kOutput, calls=%fused_computation.81 | convolution fusion | flops 1207959552 | bytes 7077888 | tf_op jit(solution)/shard_map/dot_general | solution.py:68
  12.6 1.1 fusion.51
  13.8 1.1 fusion.50
  15.1 4.6 %fusion.1 = (s32[128]{0:T(128)S(1)}, s32[128]{0:T(128)S(1)}) fusion(s32[128]{0:T(128)S(1)} %iota_add_fusion, s32[256,96]{1,0:T(8,128)S(1)} %copy.62), kind=kLoop, calls=%fused_computation.6 | loop fusion | flops 15728384 | bytes 99840 | tf_op jit(solution)/shard_map/reduce_sum | solution.py:91
  19.6 4.5 %compare_reduce_fusion = pred[128]{0:T(512)(128)(4,1)S(1)} fusion(s32[128]{0:T(128)S(1)} %iota_add_fusion, s32[256,96]{1,0:T(8,128)S(1)} %copy.62), kind=kLoop, calls=%fused_computation.3 | loop fusion | flops 6291328 | bytes 98944 | tf_op jit(solution)/shard_map/reduce_or | solution.py:88
  24.2 1.3 gather_fusion
  25.7 0.2 fusion.38
  26.0 17.5 %reduce-scatter.5.cloned.1.call-done = f32[64,1536]{1,0:T(8,128)} async-done(((f32[256,1536]{1,0:T(8,128)}), f32[64,1536]{1,0:T(8,128)}) %reduce-scatter.5.cloned.1.call-update) | async-done | bytes 393232 | tf_op jit(solution)/shard_map/reduce_scatter | solution.py:73
  43.4 1.1 reshape.358
  44.6 0.2 subtract_convert_fusion
  44.8 0.2 pad_maximum_fusion.1
  45.1 8.0 %all_gather.6 = bf16[256,2,6,128]{3,1,2,0:T(2,128)(2,1)S(1)} all-gather(bf16[64,2,6,128]{3,1,2,0:T(2,128)(2,1)S(1)} %copy.63), channel_id=1, replica_groups=mesh['grp'=2,'kvp'=4,'tp'=4] {'kvp'}, dimensions={0}, use_global_device_ids=true | all-gather | bytes 983040 | tf_op jit(solution)/shard_map/all_gather | solution.py:85
  53.2 0.9 copy-done.2
  54.1 1.4 gather_fusion.1
  55.5 7.0 %fusion.48 = (f32[128,2,6]{2,1,0:T(2,128)S(1)}, f32[128,2,6,128]{3,2,1,0:T(8,128)S(1)}) fusion(bf16[2,128,128,128]{3,2,1,0:T(8,128)(2,1)} %param.14, bf16[128,2,6,128]{3,1,2,0:T(2,128)(2,1)S(1)} %gather_fusion.1, pred[128,128]{1,0:T(8,128)(4,1)S(1)} %fusion.31), kind=kOutput, calls=%fused_computation.80 | convolution fusion | flops 50919936 | bytes 9590784 | tf_op jit(solution)/shard_map/phgd,hptd->phgt/dot_general | solution.py:98
  62.5 0.8 fusion.15
  63.4 0.5 select_reduce_fusion
  63.9 0.9 multiply_reduce_fusion
  64.9 0.2 copy.78
  65.1 1.0 reshape.382
  66.0 3.4 %all-to-all-start.2 = ((f32[4,1,768]{2,1,0:T(1,128)}), f32[4,1,768]{2,1,0:T(1,128)S(1)}, u32[]{:S(2)}, u32[]{:S(2)}) async-start(f32[4,1,768]{2,1,0:T(1,128)} %reshape.382), calls=%async_computation.5 | async-start | bytes 24576 | tf_op jit(solution)/shard_map/all_to_all | solution.py:120
  69.5 4.7 %fusion.2 = f32[128,2,6,128]{3,2,1,0:T(8,128)S(1)} fusion(bf16[2,128,128,128]{3,2,1,0:T(8,128)(2,1)} %param.15, f32[128,2,6,128]{3,2,1,0:T(8,128)S(1)} %get-tuple-element.23, f32[128,2,6]{2,1,0:T(2,128)S(1)} %get-tuple-element.22, pred[128,128]{1,0:T(8,128)(4,1)S(1)} %fusion.31), kind=kOutput, calls=%fused_computation.7 | convolution fusion | flops 50921472 | bytes 9984000 | tf_op jit(solution)/shard_map/phgt,hptd->phgd/dot_general | solution.py:105
  74.2 2.2 %fusion.8 = f32[1,256,2,6,128]{1,4,3,2,0:T(8,128)S(1)} fusion(f32[128,2,6,128]{3,2,1,0:T(8,128)S(1)} %fusion.2, f32[256,2,6]{0,2,1:T(8,128)S(1)} %select_reduce_fusion, f32[128,2,6]{0,2,1:T(8,128)S(1)} %copy.66, pred[256,128]{1,0:T(8,128)(4,1)S(1)} %fusion.29), kind=kOutput, calls=%fused_computation.18 | convolution fusion | flops 604766208 | bytes 2410496 | tf_op jit(solution)/shard_map/bphg,phgd->bhgd/dot_general | solution.py:116
  76.4 1.4 slice_bitcast_fusion.3
  77.8 0.2 copy.67
  78.0 1.0 reshape.380
  78.9 3.2 %all-to-all-start = ((f32[4,1,768]{2,1,0:T(1,128)}), f32[4,1,768]{2,1,0:T(1,128)S(1)}, u32[]{:S(2)}, u32[]{:S(2)}) async-start(f32[4,1,768]{2,1,0:T(1,128)} %reshape.380), calls=%async_computation.1 | async-start | bytes 24576 | tf_op jit(solution)/shard_map/all_to_all | solution.py:119
  82.2 3.0 %pad_maximum_fusion = f32[4,1,64,2,6,128]{2,5,4,3,1,0:T(8,128)} fusion(f32[1,1,64,2,6,128]{2,5,4,3,1,0:T(8,128)S(1)} %get-tuple-element.13, f32[1,1,64,2,6,128]{2,5,4,3,1,0:T(8,128)S(1)} %get-tuple-element.14, f32[1,1,64,2,6,128]{2,5,4,3,1,0:T(8,128)} %get-tuple-element.15, f32[1,1,64,2,6,128]{2,5,4,3,1,0:T(8,128)S(1)} %get-tuple-element.12), kind=kLoop, calls=%fused_computation.11 | loop fusion | flops 1179648 | bytes 3145728 | tf_op jit(solution)/shard_map/stack | solution.py:14
  85.3 3.2 %copy.73 = f32[4,1,64,2,6,128]{5,2,4,3,1,0:T(8,128)} copy(f32[4,1,64,2,6,128]{2,5,4,3,1,0:T(8,128)} %pad_maximum_fusion) | data formatting | bytes 3145728 | tf_op jit(solution)/shard_map/stack | solution.py:14
  88.5 3.6 %all-to-all-start.1 = ((f32[4,1,64,2,6,128]{5,2,4,3,1,0:T(8,128)}), f32[4,1,64,2,6,128]{5,2,4,3,1,0:T(8,128)S(1)}, u32[]{:S(2)}, u32[]{:S(2)}) async-start(f32[4,1,64,2,6,128]{5,2,4,3,1,0:T(8,128)} %copy.73), calls=%async_computation.3 | async-start | bytes 3145728 | tf_op jit(solution)/shard_map/all_to_all | solution.py:14
  92.1 0.8 convert_convert_fusion
  93.1 0.9 reshape.359
  94.3 1.1 constant_dynamic-slice_fusion
  95.3 0.3 fusion.27
  95.7 0.5 broadcast.311
  96.2 0.7 reduce
  96.9 0.4 reshape.383
  97.5 0.7 reduce.1
  98.2 0.4 reshape.381
  98.7 0.2 reduce_max.29
  99.1 12.9 %all-to-all-done.1 = f32[4,1,64,2,6,128]{5,2,4,3,1,0:T(8,128)S(1)} async-done(((f32[4,1,64,2,6,128]{5,2,4,3,1,0:T(8,128)}), f32[4,1,64,2,6,128]{5,2,4,3,1,0:T(8,128)S(1)}, u32[]{:S(2)}, u32[]{:S(2)}) %all-to-all-start.1) | async-done | bytes 1572896 | tf_op jit(solution)/shard_map/all_to_all | solution.py:14
  112.1 0.5 fusion.6
  112.5 0.3 copy.90
  113.1 7.9 %all_gather.7 = bf16[256,1536]{1,0:T(8,128)(2,1)S(1)} all-gather(bf16[64,1536]{1,0:T(8,128)(2,1)S(1)} %copy.88), channel_id=1, replica_groups=mesh['grp'=2,'kvp'=4,'tp'=4] {'kvp'}, dimensions={0}, use_global_device_ids=true | all-gather | bytes 983040 | tf_op jit(solution)/shard_map/all_gather | solution.py:127
  121.0 4.9 %fusion.52 = f32[256,1536]{1,0:T(8,128)} fusion(bf16[256,1536]{1,0:T(8,128)(2,1)S(1)} %all_gather.7, bf16[1536,1536]{1,0:T(8,128)(2,1)} %param.13), kind=kOutput, calls=%fused_computation.84 | convolution fusion | flops 1207959552 | bytes 7077888 | tf_op jit(solution)/shard_map/dot_general | solution.py:126
  125.9 36.3 %reduce-scatter.11.cloned.1.call-done = f32[64,1536]{1,0:T(8,128)} async-done(((f32[256,1536]{1,0:T(8,128)}), f32[64,1536]{1,0:T(8,128)}) %reduce-scatter.11.cloned.1.call-update) | async-done | bytes 393232 | tf_op jit(solution)/shard_map/reduce_scatter | solution.py:131
  162.2 1.7 convert_element_type.53
  (52 shorter events, 2.1 us)
Async XLA Ops:
  6.5 1.1 copy-start
  6.5 6.1 %copy-start.3 = (bf16[1536,256]{1,0:T(8,128)(2,1)S(1)}, bf16[1536,256]{1,0:T(8,128)(2,1)}, u32[]{:S(2)}) copy-start(bf16[1536,256]{1,0:T(8,128)(2,1)} %param.12) | copy-start | bytes 2359300
  6.5 36.9 %reduce-scatter.5.cloned.1.call-start = ((), (), s32[]{:S(2)}) async-start(), calls=%async_computation.7 | async-start | bytes 1966080 | tf_op jit(solution)/shard_map/reduce_scatter | solution.py:73
  12.5 1.2 copy-start.4
  12.5 2.4 %copy-start.5 = (s32[256,96]{0,1:T(8,128)S(1)}, s32[256,96]{0,1:T(8,128)}, u32[]{:S(2)}) copy-start(s32[256,96]{0,1:T(8,128)} %param.17) | copy-start | bytes 294916
  12.5 11.6 %copy-start.1 = (s32[256]{0:T(256)S(1)}, s32[256]{0:T(256)}, u32[]{:S(2)}) copy-start(s32[256]{0:T(256)} %param.16) | copy-start | bytes 3076
  12.6 79.5 %reduce-scatter.9.cloned.1.call-start = ((), (), s32[]{:S(2)}) async-start(), calls=%async_computation.9 | async-start | bytes 327680 | tf_op jit(solution)/shard_map/reduce_scatter | solution.py:75
  13.7 79.3 %reduce-scatter.7.cloned.1.call-start = ((), (), s32[]{:S(2)}) async-start(), calls=%async_computation.8 | async-start | bytes 327680 | tf_op jit(solution)/shard_map/reduce_scatter | solution.py:74
  53.2 0.9 copy-start.2
  66.0 12.9 %all-to-all-start.2 = ((f32[4,1,768]{2,1,0:T(1,128)}), f32[4,1,768]{2,1,0:T(1,128)S(1)}, u32[]{:S(2)}, u32[]{:S(2)}) async-start(f32[4,1,768]{2,1,0:T(1,128)} %reshape.382), calls=%async_computation.5 | async-start | bytes 24576 | tf_op jit(solution)/shard_map/all_to_all | solution.py:120
  78.9 9.5 %all-to-all-start = ((f32[4,1,768]{2,1,0:T(1,128)}), f32[4,1,768]{2,1,0:T(1,128)S(1)}, u32[]{:S(2)}, u32[]{:S(2)}) async-start(f32[4,1,768]{2,1,0:T(1,128)} %reshape.380), calls=%async_computation.1 | async-start | bytes 24576 | tf_op jit(solution)/shard_map/all_to_all | solution.py:119
  88.5 23.6 %all-to-all-start.1 = ((f32[4,1,64,2,6,128]{5,2,4,3,1,0:T(8,128)}), f32[4,1,64,2,6,128]{5,2,4,3,1,0:T(8,128)S(1)}, u32[]{:S(2)}, u32[]{:S(2)}) async-start(f32[4,1,64,2,6,128]{5,2,4,3,1,0:T(8,128)} %copy.73), calls=%async_computation.3 | async-start | bytes 3145728 | tf_op jit(solution)/shard_map/all_to_all | solution.py:14
  92.0 70.2 %reduce-scatter.11.cloned.1.call-start = ((), (), s32[]{:S(2)}) async-start(), calls=%async_computation.10 | async-start | bytes 1966080 | tf_op jit(solution)/shard_map/reduce_scatter | solution.py:131
Sparse Core Ops, SparseCore 0:
  12.7 30.6 reduce-scatter.4
  45.9 20.0 reduce-scatter.8
  68.5 20.0 reduce-scatter.6
  126.1 36.0 reduce-scatter.10
